TPU v7x, 256 devices: a whole 4x4x8 slice. The times are simulated.
256 devices in a mesh: seq: 64 (over z, y, core), head: 4 (over x).
Axes of the slice: x: 4, y: 4, z: 8, core: 2. Of those that a mesh axis runs over, the one named last changes fastest.
Arguments:
- query: bfloat16 [128, 32, 128], P(None, 'head'), may hold values from -8 to 8
- key_cache: bfloat16 [131072, 16, 128], P('seq', 'head'), may hold values from -6 to 6
- value_cache: bfloat16 [131072, 16, 128], P('seq', 'head'), may hold values from -6 to 6
- lengths: int32 [64], P('seq'), may hold values from 1 to 2048, 98304 in all
- out_weight: bfloat16 [4608, 4096], P('seq', 'head'), may hold values from -10 to 10
- norm_gain: float32 [4608], P('seq'), may hold values from 0.1 to 1.9
Outputs:
- normed: bfloat16 [128, 4608], P(None, 'seq')
Inputs may be any that keep to these rules, and one draw needn't show every extreme that they name: `lengths`: every block has at least one valid position, and some block is valid throughout.
All inputs are finite; a program needn't handle non-finite values.
Results may differ from a plain program's by a relative error of at most 0.0083.
Values may be sent and summed in bfloat16 or wider, within the bound.
A program may use at most 128 MiB of HBM per device.

v0:
```python
import jax
import jax.numpy as jnp
from jax import lax
from jax.sharding import PartitionSpec as P

D = 4608
QPRE = 144


def sent_to_all(value, axis):
    length = lax.axis_size(axis)
    return lax.all_to_all(
        jnp.broadcast_to(value[None], (length, *value.shape)), axis, 0, 0, tiled=True
    )


def over_copies(value, axis):
    everything = sent_to_all(value, axis)
    return jnp.max(everything, axis=0)


def taken_together(value, axis):
    everything = sent_to_all(value, axis)
    return jnp.sum(everything, axis=0)


def in_blocks(value, dim, length):
    lengths = value.shape
    parts = value.reshape(*lengths[:dim], length, lengths[dim] // length, *lengths[dim + 1 :])
    return jnp.moveaxis(parts, dim, 0)


def summed_on_arrival(value, axis, dim):
    parts = in_blocks(value, dim, lax.axis_size(axis))
    arrived = lax.all_to_all(parts, axis, split_axis=0, concat_axis=0, tiled=True)
    return arrived.astype(jnp.float32).sum(axis=0)


def joined_along(parts, dim):
    lengths = list(parts.shape[1:])
    lengths[dim] *= parts.shape[0]
    return jnp.moveaxis(parts, 0, dim).reshape(lengths)


def gathered_copies(value, axis, dim):
    return joined_along(sent_to_all(value, axis), dim)


def body(query, key_cache, value_cache, lengths, out_weight, norm_gain):
    tok_count, heads_local, head_dim = query.shape
    key_count, kv_local, unused_dim = key_cache.shape
    group_size = heads_local // kv_local
    score_scale = float(QPRE) ** (-0.5)
    grouped = query.reshape(tok_count, kv_local, group_size, head_dim)
    scores = (
        jnp.einsum("tkgd,ckd->kgtc", grouped, key_cache, preferred_element_type=jnp.float32)
        * score_scale
    )
    inside = lax.iota(jnp.int32, key_count) < lengths[0]
    scores = jnp.where(inside, scores, jnp.float32(-1e30))
    block_max = jnp.max(scores, axis=-1)
    weights = jnp.where(inside, jnp.exp(scores - block_max[..., None]), jnp.float32(0.0))
    block_sum = jnp.sum(weights, axis=-1)
    weights_low = weights.astype(jnp.bfloat16)
    weighted = jnp.einsum(
        "kgtc,ckd->tkgd", weights_low, value_cache, preferred_element_type=jnp.float32
    )
    weighted = weighted.reshape(tok_count, heads_local, head_dim)
    block_max = jnp.transpose(block_max, (2, 0, 1)).reshape(tok_count, heads_local)
    block_sum = jnp.transpose(block_sum, (2, 0, 1)).reshape(tok_count, heads_local)
    peak_all = over_copies(block_max, "seq")
    factor = jnp.exp(block_max - peak_all)
    total_all = taken_together(factor * block_sum, "seq")
    scaled = (weighted * factor[..., None]).reshape(tok_count, heads_local * head_dim)
    share = summed_on_arrival(scaled.astype(jnp.bfloat16), "seq", 1)
    share_width = share.shape[1]
    first_col = lax.axis_index("seq") * share_width
    column_head = (first_col + lax.iota(jnp.int32, share_width)) // head_dim
    selector = (lax.iota(jnp.int32, heads_local)[:, None] == column_head[None, :]).astype(
        jnp.float32
    )
    column_total = jnp.dot(total_all, selector, precision=lax.Precision.HIGHEST)
    attention_share = (share / column_total).astype(jnp.bfloat16)
    attention = gathered_copies(attention_share, "seq", 1)
    projected_part = lax.dot_general(
        attention, out_weight, (((1,), (1,)), ((), ())), preferred_element_type=jnp.float32
    )
    projected = taken_together(projected_part, "head")
    square_part = jnp.sum(projected * projected, axis=-1)
    square_total = taken_together(square_part, "seq")
    mean_square = square_total / D
    normed = projected * lax.rsqrt(mean_square + 1e-06)[:, None] * norm_gain[None, :]
    return normed.astype(jnp.bfloat16)


def solution(mesh):
    placed = (
        P(None, "head", None),
        P("seq", "head", None),
        P("seq", "head", None),
        P("seq"),
        P("seq", "head"),
        P("seq"),
    )
    return jax.shard_map(
        body, mesh=mesh, in_specs=placed, out_specs=P(None, "seq"), check_vma=False
    )
```

profile of v0, /device:TPU:1, one launch (start us, length us, event | category | flops | bytes accessed | tf_op | source)
XLA Modules:
  0.0 117.1 jit_solution(12879919024105896091)
XLA Ops:
  0.0 0.0 copy-start
  0.0 0.0 copy-start.3
  0.8 0.1 copy-done
  1.0 6.2 %bitcast_reduce_fusion = (f32[4,2,128]{2,1,0:T(2,128)S(1)}, f32[4,2048,128,2]{2,1,3,0:T(8,128)}) fusion(pred[2048]{0:T(1024)(128)(4,1)S(1)} %iota_compare_fusion, bf16[128,4,2,128]{3,2,1,0:T(2,128)(2,1)S(1)} %bitcast.37, bf16[2048,4,128,1]{2,1,0,3:T(4,128)(2,1)} %bitcast.44), kind=kOutput, calls=%fused_computation.1 | convolution fusion | flops 543161344 | bytes 10754048 | tf_op jit(solution)/shard_map/tkgd,ckd->kgtc/dot_general | solution.py:56
  7.1 0.7 broadcast_in_dim.28
  7.9 13.1 %all-to-all-start = ((f32[64,128,8]{1,2,0:T(8,128)}), f32[64,128,8]{1,2,0:T(8,128)S(1)}, u32[]{:S(2)}, u32[]{:S(2)}) async-start(f32[64,128,8]{1,2,0:T(8,128)} %broadcast_in_dim.28), calls=%async_computation | async-start | bytes 524288 | tf_op jit(solution)/shard_map/all_to_all | solution.py:12
  21.0 0.0 copy-done.3
  21.0 6.4 %fusion.4 = f32[4,2,128,128]{2,3,1,0:T(8,128)S(1)} fusion(f32[4,2048,128,2]{2,1,3,0:T(8,128)} %get-tuple-element.8, f32[4,2,128]{2,1,0:T(2,128)S(1)} %get-tuple-element.7, pred[2048]{0:T(1024)(128)(4,1)S(1)} %iota_compare_fusion, bf16[2048,4,128,1]{2,1,0,3:T(4,128)(2,1)S(1)} %bitcast.45), kind=kOutput, calls=%fused_computation.7 | convolution fusion | flops 547356672 | bytes 11016192 | tf_op jit(solution)/shard_map/kgtc,ckd->tkgd/dot_general | solution.py:65
  27.4 0.0 copy-start.1
  27.4 0.0 copy-start.2
  27.4 4.6 %fusion.2 = f32[4,2,128]{2,1,0:T(2,128)S(1)} fusion(f32[4,2048,128,2]{2,1,3,0:T(8,128)} %get-tuple-element.8, f32[4,2,128]{2,1,0:T(2,128)S(1)} %get-tuple-element.7, pred[2048]{0:T(1024)(128)(4,1)S(1)} %iota_compare_fusion), kind=kLoop, calls=%fused_computation.5 | loop fusion | flops 10484736 | bytes 8398848 | tf_op jit(solution)/shard_map/reduce_sum | solution.py:63
  32.1 2.0 %all-to-all-done = f32[64,128,8]{1,2,0:T(8,128)S(1)} async-done(((f32[64,128,8]{1,2,0:T(8,128)}), f32[64,128,8]{1,2,0:T(8,128)S(1)}, u32[]{:S(2)}, u32[]{:S(2)}) %all-to-all-start) | async-done | bytes 262176 | tf_op jit(solution)/shard_map/all_to_all | solution.py:12
  34.1 0.1 reduce_max.19
  34.2 0.1 fusion.12
  34.2 21.2 %all_to_all.31 = bf16[64,128,16]{1,2,0:T(8,128)(2,1)S(1)} all-to-all(bf16[64,128,16]{1,2,0:T(8,128)(2,1)S(1)} %fusion.12), channel_id=1, replica_groups=mesh['seq'=64,'head'=4] {'seq'}, dimensions={0} | all-to-all | bytes 524288 | tf_op jit(solution)/shard_map/all_to_all | solution.py:35
  55.4 0.7 broadcast_in_dim.54
  56.1 4.8 %all-to-all-start.2 = ((f32[64,128,8]{1,2,0:T(8,128)}), f32[64,128,8]{1,2,0:T(8,128)S(1)}, u32[]{:S(2)}, u32[]{:S(2)}) async-start(f32[64,128,8]{1,2,0:T(8,128)} %broadcast_in_dim.54), calls=%async_computation.2 | async-start | bytes 524288 | tf_op jit(solution)/shard_map/all_to_all | solution.py:12
  60.9 0.1 convert_reduce_fusion
  61.0 13.0 %all-to-all-done.2 = f32[64,128,8]{1,2,0:T(8,128)S(1)} async-done(((f32[64,128,8]{1,2,0:T(8,128)}), f32[64,128,8]{1,2,0:T(8,128)S(1)}, u32[]{:S(2)}, u32[]{:S(2)}) %all-to-all-start.2) | async-done | bytes 262176 | tf_op jit(solution)/shard_map/all_to_all | solution.py:12
  74.0 0.1 reduce_sum.56
  74.0 0.2 fusion.11
  74.3 17.6 %all_to_all.32 = bf16[64,128,16]{1,2,0:T(8,128)(2,1)S(1)} all-to-all(bf16[64,128,16]{1,2,0:T(8,128)(2,1)S(1)} %broadcast_in_dim.55), channel_id=1, replica_groups=mesh['seq'=64,'head'=4] {'seq'}, dimensions={0} | all-to-all | bytes 524288 | tf_op jit(solution)/shard_map/all_to_all | solution.py:12
  91.9 0.0 copy-done.1
  91.9 0.2 fusion.19
  92.1 8.8 %all_to_all.33 = f32[4,128,72]{1,2,0:T(8,128)S(1)} all-to-all(f32[4,128,72]{1,2,0:T(8,128)S(1)} %broadcast_in_dim.56), channel_id=1, replica_groups=mesh['seq'=64,'head'=4] {'head'}, dimensions={0} | all-to-all | bytes 294912 | tf_op jit(solution)/shard_map/all_to_all | solution.py:12
  101.0 15.3 %all_to_all.34 = f32[64,1,128]{2,1,0:T(1,128)S(1)} all-to-all(f32[64,1,128]{2,1,0:T(1,128)S(1)} %broadcast_in_dim.57), channel_id=1, replica_groups=mesh['seq'=64,'head'=4] {'seq'}, dimensions={0} | all-to-all | bytes 65536 | tf_op jit(solution)/shard_map/all_to_all | solution.py:12
  116.4 0.0 copy-done.2
  116.4 0.7 multiply_convert_fusion.1
  (11 shorter events, 0.2 us)
Async XLA Ops:
  0.0 1.0 copy-start
  0.0 21.0 %copy-start.3 = (bf16[2048,4,128]{2,1,0:T(4,128)(2,1)S(1)}, bf16[2048,4,128]{2,1,0:T(4,128)(2,1)}, u32[]{:S(2)}) copy-start(bf16[2048,4,128]{2,1,0:T(4,128)(2,1)} %param.8) | copy-start | bytes 6291460
  7.9 26.2 %all-to-all-start = ((f32[64,128,8]{1,2,0:T(8,128)}), f32[64,128,8]{1,2,0:T(8,128)S(1)}, u32[]{:S(2)}, u32[]{:S(2)}) async-start(f32[64,128,8]{1,2,0:T(8,128)} %broadcast_in_dim.28), calls=%async_computation | async-start | bytes 524288 | tf_op jit(solution)/shard_map/all_to_all | solution.py:12
  27.4 64.5 %copy-start.1 = (bf16[72,1024]{1,0:T(8,128)(2,1)S(1)}, bf16[72,1024]{1,0:T(8,128)(2,1)}, u32[]{:S(2)}) copy-start(bf16[72,1024]{1,0:T(8,128)(2,1)} %param.10) | copy-start | bytes 442372
  27.4 89.0 %copy-start.2 = (f32[72]{0:T(128)S(1)}, f32[72]{0:T(128)}, u32[]{:S(2)}) copy-start(f32[72]{0:T(128)} %param.11) | copy-start | bytes 868
  56.1 17.9 %all-to-all-start.2 = ((f32[64,128,8]{1,2,0:T(8,128)}), f32[64,128,8]{1,2,0:T(8,128)S(1)}, u32[]{:S(2)}, u32[]{:S(2)}) async-start(f32[64,128,8]{1,2,0:T(8,128)} %broadcast_in_dim.54), calls=%async_computation.2 | async-start | bytes 524288 | tf_op jit(solution)/shard_map/all_to_all | solution.py:12
where the time goes:
time: 118 us; the launch traced here: 117 us
  blocking collectives  62.9 us (53%)
  starting transfers between devices  17.9 us (15%)
  waiting for transfers between devices  15 us (13%)
  matrix products  12.9 us (11%)
  other arithmetic  5.68 us (5%)
  local copies, waits for them, and re-layouts  1.67 us (1%)
    all_to_all x3, blocking collectives, sent_to_all(): lax.all_to_all(jnp.broadcast_to(value[None], (length, *value.shape)), axi...  41.8 us
    all_to_all x1, blocking collectives, summed_on_arrival(): lax.all_to_all(parts, axis, split_axis=0, concat_axis=0, tiled=True)  21.2 us
    all_to_all x2, starting transfers between devices, sent_to_all(): lax.all_to_all(jnp.broadcast_to(value[None], (length, *value.shape)), axi...  17.9 us
    all_to_all x2, waiting for transfers between devices, sent_to_all(): lax.all_to_all(jnp.broadcast_to(value[None], (length, *value.shape)), axi...  15 us
    dot_general x1, matrix products, body(): jnp.einsum('kgtc,ckd->tkgd', weights_low, value_cache, preferred_element_...  6.38 us
    dot_general x1, matrix products, body(): jnp.einsum('tkgd,ckd->kgtc', grouped, key_cache, preferred_element_type=j...  6.18 us
    reduce_sum x1, other arithmetic, body(): block_sum = jnp.sum(weights, axis=-1)  4.62 us
  transfers between devices with their start and end apart: 2, of which 2 were waited for; matrix products, arithmetic and copies ran while one was open for 9% of the time, Pallas kernels for 0%

commit v1 on v0

v1 whole, which is shorter than its diff:
```python
import functools

import jax
import jax.numpy as jnp
from jax import lax
from jax.experimental import pallas as pl
from jax.experimental.pallas import tpu as pltpu
from jax.sharding import PartitionSpec as P

D = 4608
QPRE = 144
NZ = 8
NJ = 8
NX = 4
HD = 128
TOK = 128
ROWS = 72
DZ = HD // NZ
MESH = pl.DeviceIdType.MESH


def kernel(
    acc_ref,
    stat_ref,
    weight_ref,
    out_ref,
    got1,
    gstat1,
    weights,
    send2,
    sstat2,
    got2,
    gstat2,
    attn,
    send4,
    got4,
    got5,
    got6,
    got7,
    s1,
    r1,
    t1,
    q1,
    sw,
    rw,
    s2,
    r2,
    t2,
    q2,
    s3,
    r3,
    s4,
    r4,
    s5,
    r5,
    s6,
    r6,
    s7,
    r7,
):
    seq = lax.axis_index("seq")
    x = lax.axis_index("head")
    j = lax.rem(seq, NJ)
    z = lax.div(seq, NJ)

    def peer_j(k):
        return lax.rem(j + k, NJ)

    def peer_z(k):
        return lax.rem(z + k, NZ)

    def peer_x(k):
        return lax.rem(x + k, NX)

    def at_j(p):
        return (z * NJ + p, x)

    def at_z(p):
        return (p * NJ + j, x)

    def at_x(p):
        return (seq, p)

    barrier = pltpu.get_barrier_semaphore()
    for k in range(1, NJ):
        pl.semaphore_signal(barrier, inc=1, device_id=at_j(peer_j(k)), device_id_type=MESH)
    for k in range(1, NZ):
        pl.semaphore_signal(barrier, inc=1, device_id=at_z(peer_z(k)), device_id_type=MESH)
    for k in range(1, NX):
        pl.semaphore_signal(barrier, inc=1, device_id=at_x(peer_x(k)), device_id_type=MESH)
    pl.semaphore_wait(barrier, NJ + NZ + NX - 3)

    def copy(src, dst, ssem, rsem, device):
        return pltpu.make_async_remote_copy(
            src_ref=src, dst_ref=dst, send_sem=ssem, recv_sem=rsem, device_id=device, device_id_type=MESH
        )

    far_j = (4, 3, 5, 2, 6, 1, 7)
    far_z = (4, 3, 5, 2, 6, 1, 7)
    sends = []

    def exchange(src, dst, ssem, rsem, mine, order, peer, place):
        for k in order:
            p = peer(k)
            c = copy(src(p), dst.at[mine], ssem.at[k], rsem.at[mine], place(p))
            c.start()
            sends.append(c)

    def arrived(src, dst, ssem, rsem, order, peer, place):
        for k in order:
            p = peer(k)
            copy(src, dst.at[p], ssem.at[k], rsem.at[p], place(p)).wait_recv()

    exchange(lambda p: stat_ref.at[p], gstat1, t1, q1, j, far_j, peer_j, at_j)
    exchange(lambda p: acc_ref.at[p], got1, s1, r1, j, far_j, peer_j, at_j)
    exchange(
        lambda p: weight_ref.at[:, pl.ds(pl.multiple_of(p * HD, HD), HD)], weights, sw, rw, j, far_j, peer_j, at_j
    )
    gstat1[j] = stat_ref[j]
    got1[j] = acc_ref[j]
    weights[j] = weight_ref[:, pl.ds(pl.multiple_of(j * HD, HD), HD)]
    arrived(stat_ref.at[0], gstat1, t1, q1, far_j[::-1], peer_j, at_j)
    arrived(acc_ref.at[0], got1, s1, r1, far_j[::-1], peer_j, at_j)

    def merged(got, gstat, count):
        tops = [gstat[p, 0:1, :] for p in range(count)]
        top = functools.reduce(jnp.maximum, tops)
        total, value = None, None
        for p in range(count):
            factor = jnp.exp(tops[p] - top)
            one = factor * gstat[p, 1:2, :]
            many = factor * got[p].astype(jnp.float32)
            total = one if total is None else total + one
            value = many if value is None else value + many
        return top, total, value

    top, total, value = merged(got1, gstat1, NJ)
    sstat2[0:1, :] = top
    sstat2[1:2, :] = total
    for p in range(NZ):
        send2[p] = value[p * DZ : (p + 1) * DZ, :].astype(jnp.bfloat16)

    exchange(lambda p: sstat2, gstat2, t2, q2, z, far_z, peer_z, at_z)
    exchange(lambda p: send2.at[p], got2, s2, r2, z, far_z, peer_z, at_z)
    gstat2[z] = sstat2[...]
    got2[z] = send2[z]
    arrived(sstat2, gstat2, t2, q2, far_z[::-1], peer_z, at_z)
    arrived(send2.at[0], got2, s2, r2, far_z[::-1], peer_z, at_z)
    top, total, value = merged(got2, gstat2, NZ)
    attn[z] = (value / total).astype(jnp.bfloat16)

    exchange(lambda p: attn.at[z], attn, s3, r3, z, far_z, peer_z, at_z)
    arrived(weight_ref.at[:, pl.ds(0, HD)], weights, sw, rw, far_j[::-1], peer_j, at_j)
    arrived(attn.at[0], attn, s3, r3, far_z[::-1], peer_z, at_z)

    whole = jnp.concatenate([attn[p] for p in range(NZ)], axis=0)
    for p in range(NJ):
        send4[p] = jnp.dot(weights[p], whole, preferred_element_type=jnp.float32).astype(jnp.bfloat16)
    exchange(lambda p: send4.at[p], got4, s4, r4, j, far_j, peer_j, at_j)
    got4[j] = send4[j]
    arrived(send4.at[0], got4, s4, r4, far_j[::-1], peer_j, at_j)
    part = functools.reduce(jnp.add, [got4[p].astype(jnp.float32) for p in range(NJ)])

    got5[x] = part.astype(jnp.bfloat16)
    exchange(lambda p: got5.at[x], got5, s5, r5, x, (2, 1, 3), peer_x, at_x)
    arrived(got5.at[0], got5, s5, r5, (1, 3, 2), peer_x, at_x)
    projected = functools.reduce(jnp.add, [got5[p].astype(jnp.float32) for p in range(NX)])

    got6[j] = jnp.sum(projected * projected, axis=0, keepdims=True)
    exchange(lambda p: got6.at[j], got6, s6, r6, j, far_j, peer_j, at_j)
    arrived(got6.at[0], got6, s6, r6, far_j[::-1], peer_j, at_j)
    got7[z] = functools.reduce(jnp.add, [got6[p] for p in range(NJ)])
    exchange(lambda p: got7.at[z], got7, s7, r7, z, far_z, peer_z, at_z)
    arrived(got7.at[0], got7, s7, r7, far_z[::-1], peer_z, at_z)
    square = functools.reduce(jnp.add, [got7[p] for p in range(NZ)])
    out_ref[...] = projected * lax.rsqrt(square * (1.0 / D) + 1e-06)

    for c in sends:
        c.wait_send()


def communicate(acc, stat, weight):
    bf16, f32 = jnp.bfloat16, jnp.float32
    dma = pltpu.SemaphoreType.DMA
    j2, z2, x2 = [dma((NJ,))] * 2, [dma((NZ,))] * 2, [dma((NX,))] * 2
    vmem = pl.BlockSpec(memory_space=pltpu.VMEM)
    return pl.pallas_call(
        kernel,
        out_shape=jax.ShapeDtypeStruct((ROWS, TOK), f32),
        in_specs=[vmem] * 3,
        out_specs=vmem,
        scratch_shapes=[
            pltpu.VMEM((NJ, HD, TOK), bf16),
            pltpu.VMEM((NJ, 2, TOK), f32),
            pltpu.VMEM((NJ, ROWS, HD), bf16),
            pltpu.VMEM((NZ, DZ, TOK), bf16),
            pltpu.VMEM((2, TOK), f32),
            pltpu.VMEM((NZ, DZ, TOK), bf16),
            pltpu.VMEM((NZ, 2, TOK), f32),
            pltpu.VMEM((NZ, DZ, TOK), bf16),
            pltpu.VMEM((NJ, ROWS, TOK), bf16),
            pltpu.VMEM((NJ, ROWS, TOK), bf16),
            pltpu.VMEM((NX, ROWS, TOK), bf16),
            pltpu.VMEM((NJ, 1, TOK), f32),
            pltpu.VMEM((NZ, 1, TOK), f32),
            *j2, *j2, *j2, *z2, *z2, *z2, *j2, *x2, *j2, *z2,
        ],
        compiler_params=pltpu.CompilerParams(collective_id=0, has_side_effects=True),
    )(acc, stat, weight)


def body(query, key_cache, value_cache, lengths, out_weight, norm_gain):
    tok_count, heads_local, head_dim = query.shape
    key_count, kv_local, unused_dim = key_cache.shape
    group_size = heads_local // kv_local
    score_scale = float(QPRE) ** (-0.5)
    grouped = query.reshape(tok_count, kv_local, group_size, head_dim)
    scores = (
        jnp.einsum("tkgd,ckd->kgtc", grouped, key_cache, preferred_element_type=jnp.float32)
        * score_scale
    )
    inside = lax.iota(jnp.int32, key_count) < lengths[0]
    scores = jnp.where(inside, scores, jnp.float32(-1e30))
    block_max = jnp.max(scores, axis=-1)
    weights = jnp.where(inside, jnp.exp(scores - block_max[..., None]), jnp.float32(0.0))
    block_sum = jnp.sum(weights, axis=-1)
    weighted = jnp.einsum(
        "kgtc,ckd->kgdt", weights.astype(jnp.bfloat16), value_cache, preferred_element_type=jnp.float32
    )
    acc = weighted.astype(jnp.bfloat16).reshape(heads_local, head_dim, tok_count)
    stat = jnp.stack([block_max, block_sum], axis=2).reshape(heads_local, 2, tok_count)
    normed = communicate(acc, stat, out_weight)
    return (normed * norm_gain[:, None]).astype(jnp.bfloat16).T


def solution(mesh):
    placed = (
        P(None, "head", None),
        P("seq", "head", None),
        P("seq", "head", None),
        P("seq"),
        P("seq", "head"),
        P("seq"),
    )
    return jax.shard_map(
        body, mesh=mesh, in_specs=placed, out_specs=P(None, "seq"), check_vma=False
    )
```

time: 118 us -> 56.8 us (0.48)
  blocking collectives: 62.9 us -> 0 us
  Pallas kernels: 0 us -> 42.1 us
  starting transfers between devices: 17.9 us -> 0 us
  waiting for transfers between devices: 15 us -> 0 us
  matrix products: 12.9 us -> 7.28 us
    all_to_all x4 -> x0, blocking collectives: 62.9 us -> none  [the longest x3 41.8 us: sent_to_all(): lax.all_to_all(jnp.broadcast_to(value[None], (length, *value.shape)), axi...]
    pallas_call x0 -> x1, Pallas kernels: none -> 42.1 us  [communicate(): pl.pallas_call(kernel, out_shape=jax.ShapeDtypeStruct((ROWS, TOK), f32),...]
    all_to_all x2 -> x0, starting transfers between devices: 17.9 us -> none  [sent_to_all(): lax.all_to_all(jnp.broadcast_to(value[None], (length, *value.shape)), axi...]
    all_to_all x2 -> x0, waiting for transfers between devices: 15 us -> none  [sent_to_all(): lax.all_to_all(jnp.broadcast_to(value[None], (length, *value.shape)), axi...]
    dot_general x3 -> x1, matrix products: 6.75 us -> 3.44 us  [body(): jnp.einsum('kgtc,ckd->kgdt', weights.astype(jnp.bfloat16), value_cache, p...]
    dot_general x1, matrix products: 6.18 us -> 3.84 us  [body(): jnp.einsum('tkgd,ckd->kgtc', grouped, key_cache, preferred_element_type=j...]
    reduce_sum x1, other arithmetic: 4.62 us -> 2.65 us  [body(): block_sum = jnp.sum(weights, axis=-1)]
    broadcast_in_dim x5 -> x0, local copies, waits for them, and re-layouts: 1.52 us -> none  [sent_to_all(): jnp.broadcast_to(value[None], (length, *value.shape))]
  transfers between devices with their start and end apart: 2 -> 0, of which waited for: 2 -> 0; matrix products, arithmetic and copies ran while one was open for 9% -> 0% of each run, Pallas kernels for 0% -> 0%
where the time goes in v1:
time: 56.8 us; the launch traced here: 56.6 us
  Pallas kernels  42.1 us (74%)
  matrix products  7.28 us (13%)
  other arithmetic  4.72 us (8%)
  local copies, waits for them, and re-layouts  1.65 us (3%)
  between operations  0.85 us (1%)
    pallas_call x1, Pallas kernels, communicate(): pl.pallas_call(kernel, out_shape=jax.ShapeDtypeStruct((ROWS, TOK), f32),...  42.1 us
    dot_general x1, matrix products, body(): jnp.einsum('tkgd,ckd->kgtc', grouped, key_cache, preferred_element_type=j...  3.84 us
    dot_general x1, matrix products, body(): jnp.einsum('kgtc,ckd->kgdt', weights.astype(jnp.bfloat16), value_cache, p...  3.44 us
    reduce_sum x1, other arithmetic, body(): block_sum = jnp.sum(weights, axis=-1)  2.65 us
    transpose x1, other arithmetic, body(): return (normed * norm_gain[:, None]).astype(jnp.bfloat16).T  1.45 us

profile of v1, /device:TPU:1, one launch (start us, length us, event | category | flops | bytes accessed | tf_op | source)
XLA Modules:
  0.0 56.6 jit_solution(10306548360371152348)
XLA Ops:
  0.0 0.0 copy-start
  0.8 0.8 %copy-done = bf16[2048,4,128]{2,1,0:T(4,128)(2,1)S(1)} copy-done((bf16[2048,4,128]{2,1,0:T(4,128)(2,1)S(1)}, bf16[2048,4,128]{2,1,0:T(4,128)(2,1)}, u32[]{:S(2)}) %copy-start) | copy-done | bytes 2097176
  1.6 3.8 %bitcast_reduce_fusion = (f32[4,2,128]{2,1,0:T(2,128)S(1)}, f32[4,2048,128,2]{2,1,3,0:T(8,128)S(1)}) fusion(pred[2048]{0:T(1024)(128)(4,1)S(1)} %iota_compare_fusion, bf16[128,4,2,128]{3,2,1,0:T(2,128)(2,1)} %bitcast.33, bf16[2048,4,128,1]{2,1,0,3:T(4,128)(2,1)} %bitcast.32), kind=kOutput, calls=%fused_computation.1 | convolution fusion | flops 543161344 | bytes 10754048 | tf_op jit(solution)/shard_map/tkgd,ckd->kgtc/dot_general | solution.py:219
  5.5 2.6 %fusion.2 = f32[4,2,128]{2,1,0:T(2,128)S(1)} fusion(f32[4,2048,128,2]{2,1,3,0:T(8,128)S(1)} %get-tuple-element.6, f32[4,2,128]{2,1,0:T(2,128)S(1)} %get-tuple-element.5, pred[2048]{0:T(1024)(128)(4,1)S(1)} %iota_compare_fusion), kind=kLoop, calls=%fused_computation.5 | loop fusion | flops 10484736 | bytes 8398848 | tf_op jit(solution)/shard_map/reduce_sum | solution.py:226
  8.1 0.0 copy-start.1
  8.1 3.4 %fusion.16 = bf16[4,2,128,128]{2,3,1,0:T(8,128)(2,1)S(1)} fusion(bf16[2048,4,128,1]{2,1,0,3:T(4,128)(2,1)S(1)} %bitcast.28, f32[4,2048,128,2]{2,1,3,0:T(8,128)S(1)} %get-tuple-element.6, f32[4,2,128]{2,1,0:T(2,128)S(1)} %get-tuple-element.5, pred[2048]{0:T(1024)(128)(4,1)S(1)} %iota_compare_fusion), kind=kOutput, calls=%fused_computation.14 | convolution fusion | flops 547487744 | bytes 10754048 | tf_op jit(solution)/shard_map/kgtc,ckd->kgdt/dot_general | solution.py:227
  11.6 0.8 %copy.11 = bf16[4,2,128,128]{3,2,1,0:T(8,128)(2,1)} copy(bf16[4,2,128,128]{2,3,1,0:T(8,128)(2,1)S(1)} %fusion.16) | data formatting | bytes 524288 | tf_op jit(solution)/shard_map/convert_element_type | solution.py:230
  12.4 0.6 %pad_maximum_fusion.stat_ref = f32[8,2,128]{2,1,0:T(2,128)} fusion(f32[8,1,128]{2,1,0:T(1,128)S(1)} %bitcast.31, f32[8,1,128]{2,1,0:T(1,128)S(1)} %bitcast.30), kind=kLoop, calls=%fused_computation.18 | loop fusion | flops 2048 | bytes 16384 | tf_op jit(solution)/shard_map/stack | solution.py:231
  13.0 42.1 %shard_map.64 = f32[72,128]{1,0:T(8,128)} custom-call(bf16[8,128,128]{2,1,0:T(8,128)(2,1)} %bitcast.29, f32[8,2,128]{2,1,0:T(2,128)} %pad_maximum_fusion.stat_ref, bf16[72,1024]{1,0:T(8,128)(2,1)} %weight_ref.1), custom_call_target="tpu_custom_call" | custom-call | tf_op jit(solution)/shard_map/pallas_call | solution.py:187
  55.1 0.0 copy-done.1
  55.1 1.5 %fusion.22 = bf16[128,72]{0,1:T(8,128)(2,1)} fusion(f32[72,128]{1,0:T(8,128)} %shard_map.64, f32[72]{0:T(128)S(1)} %copy-done.1), kind=kLoop, calls=%fused_computation.17 | loop fusion | flops 18432 | bytes 55584 | tf_op jit(solution)/shard_map/transpose | solution.py:233
  (1 shorter events, 0.0 us)
Async XLA Ops:
  0.0 1.6 %copy-start = (bf16[2048,4,128]{2,1,0:T(4,128)(2,1)S(1)}, bf16[2048,4,128]{2,1,0:T(4,128)(2,1)}, u32[]{:S(2)}) copy-start(bf16[2048,4,128]{2,1,0:T(4,128)(2,1)} %param.8) | copy-start | bytes 6291460
  8.1 47.0 %copy-start.1 = (f32[72]{0:T(128)S(1)}, f32[72]{0:T(128)}, u32[]{:S(2)}) copy-start(f32[72]{0:T(128)} %param.11) | copy-start | bytes 868

commit v2 on v1

v2 whole, which is shorter than its diff:
```python
import functools

import jax
import jax.numpy as jnp
from jax import lax
from jax.experimental import pallas as pl
from jax.experimental.pallas import tpu as pltpu
from jax.sharding import PartitionSpec as P

D = 4608
QPRE = 144
NZ = 8
NJ = 8
NX = 4
NS = 64
HD = 128
TOK = 128
ROWS = 72
DZ = HD // NZ
KV = 4
KEYS = 2048
PARTS = 4
STEP = QPRE ** -0.5 * 1.4426950408889634
MESH = pl.DeviceIdType.MESH


def kernel(
    length_ref,
    query_ref,
    key_ref,
    value_ref,
    weight_ref,
    out_ref,
    key_low,
    value_low,
    keys,
    values,
    queries,
    acc_ref,
    stat_ref,
    got1,
    gstat1,
    weights,
    send2,
    sstat2,
    got2,
    gstat2,
    attn,
    send4,
    got4,
    got5,
    got6,
    ck,
    cv,
    cw,
    s1,
    r1,
    t1,
    q1,
    sw,
    rw,
    s2,
    r2,
    t2,
    q2,
    s3,
    r3,
    s4,
    r4,
    s5,
    r5,
    s6,
    r6,
):
    seq = lax.axis_index("seq")
    x = lax.axis_index("head")
    j = lax.rem(seq, NJ)
    z = lax.div(seq, NJ)
    y = lax.div(j, 2)

    part = KEYS * KV // PARTS
    key_copies = [
        pltpu.make_async_copy(key_ref.at[pl.ds(i * part, part)], key_low.at[pl.ds(i * part, part)], ck.at[i])
        for i in range(PARTS)
    ]
    value_copies = [
        pltpu.make_async_copy(value_ref.at[pl.ds(i * part, part)], value_low.at[pl.ds(i * part, part)], cv.at[i])
        for i in range(PARTS)
    ]
    for c in key_copies + value_copies:
        c.start()

    def peer_j(k):
        return lax.rem(j + k, NJ)

    def peer_z(k):
        return lax.rem(z + k, NZ)

    def peer_s(k):
        return lax.rem(seq + k, NS)

    def peer_x(k):
        return lax.rem(x + k, NX)

    def at_j(p):
        return (z * NJ + p, x)

    def at_z(p):
        return (p * NJ + j, x)

    def at_s(p):
        return (p, x)

    def at_x(p):
        return (seq, p)

    barrier = pltpu.get_barrier_semaphore()
    for k in range(1, NS):
        pl.semaphore_signal(barrier, inc=1, device_id=at_s(peer_s(k)), device_id_type=MESH)
    for k in range(1, NX):
        pl.semaphore_signal(barrier, inc=1, device_id=at_x(peer_x(k)), device_id_type=MESH)

    def copy(src, dst, ssem, rsem, device):
        return pltpu.make_async_remote_copy(
            src_ref=src, dst_ref=dst, send_sem=ssem, recv_sem=rsem, device_id=device, device_id_type=MESH
        )

    far_j = (4, 3, 5, 2, 6, 1, 7)
    far_z = (4, 3, 5, 2, 6, 1, 7)
    sends = []

    def exchange(src, dst, ssem, rsem, mine, order, peer, place):
        for k in order:
            p = peer(k)
            c = copy(src(p), dst.at[mine], ssem.at[k], rsem.at[mine], place(p))
            c.start()
            sends.append(c)

    def arrived(src, dst, ssem, rsem, order, peer, place):
        for k in order:
            p = peer(k)
            copy(src, dst.at[p], ssem.at[k], rsem.at[p], place(p)).wait_recv()

    queries[...] = query_ref[...].astype(jnp.float32)
    for i in range(PARTS):
        key_copies[i].wait()
        keys[i * part : (i + 1) * part, :] = key_low[i * part : (i + 1) * part, :].astype(jnp.float32)
    for i in range(PARTS):
        value_copies[i].wait()
        values[i * part : (i + 1) * part, :] = value_low[i * part : (i + 1) * part, :].astype(jnp.float32)

    pl.semaphore_wait(barrier, NS + NX - 2)
    exchange(
        lambda p: weight_ref.at[:, pl.ds(pl.multiple_of(p * HD, HD), HD)], weights, sw, rw, j, far_j, peer_j, at_j
    )
    own_weight = pltpu.make_async_copy(
        weight_ref.at[:, pl.ds(pl.multiple_of(j * HD, HD), HD)], weights.at[j], cw
    )
    own_weight.start()
    length = length_ref[0]

    def attend(h):
        key = keys[pl.ds(h, KEYS, stride=KV), :].astype(jnp.bfloat16)
        query = jnp.concatenate(
            [queries[pl.ds(2 * h + g, TOK, stride=NJ), :].astype(jnp.bfloat16) for g in range(2)], axis=0
        )
        scores = lax.dot_general(key, query, (((1,), (1,)), ((), ())), preferred_element_type=jnp.float32)
        place = lax.broadcasted_iota(jnp.int32, (KEYS, 2 * TOK), 0)
        scores = jnp.where(place < length, scores, -1e30)
        top = jnp.max(scores, axis=0, keepdims=True)
        soft = jnp.exp2((scores - top) * STEP)
        total = jnp.sum(soft, axis=0, keepdims=True)
        value = values[pl.ds(h, KEYS, stride=KV), :].astype(jnp.bfloat16)
        acc = lax.dot_general(
            value, soft.astype(jnp.bfloat16), (((0,), (0,)), ((), ())), preferred_element_type=jnp.float32
        )
        for g in range(2):
            side = slice(g * TOK, (g + 1) * TOK)
            acc_ref[2 * h + g] = acc[:, side].astype(jnp.bfloat16)
            stat_ref[2 * h + g, 0:1, :] = top[:, side] * STEP
            stat_ref[2 * h + g, 1:2, :] = total[:, side]

    def give(p):
        copy(stat_ref.at[p], gstat1.at[j], t1.at[p], q1.at[j], at_j(p)).start()
        copy(acc_ref.at[p], got1.at[j], s1.at[p], r1.at[j], at_j(p)).start()

    def remote(i, carry):
        h = lax.rem(y + 1 + i, KV)
        attend(h)
        give(2 * h)
        give(2 * h + 1)
        return carry

    lax.fori_loop(0, KV - 1, remote, 0)
    attend(y)
    give(4 * y + 1 - j)
    gstat1[j] = stat_ref[j]
    got1[j] = acc_ref[j]
    arrived(stat_ref.at[0], gstat1, t1, q1, far_j[::-1], peer_j, at_j)
    arrived(acc_ref.at[0], got1, s1, r1, far_j[::-1], peer_j, at_j)

    def merged(got, gstat, count):
        tops = [gstat[p, 0:1, :] for p in range(count)]
        top = functools.reduce(jnp.maximum, tops)
        total, value = None, None
        for p in range(count):
            factor = jnp.exp2(tops[p] - top)
            one = factor * gstat[p, 1:2, :]
            many = factor * got[p].astype(jnp.float32)
            total = one if total is None else total + one
            value = many if value is None else value + many
        return top, total, value

    top, total, value = merged(got1, gstat1, NJ)
    sstat2[0:1, :] = top
    sstat2[1:2, :] = total
    for p in range(NZ):
        send2[p] = value[p * DZ : (p + 1) * DZ, :].astype(jnp.bfloat16)

    exchange(lambda p: sstat2, gstat2, t2, q2, z, far_z, peer_z, at_z)
    exchange(lambda p: send2.at[p], got2, s2, r2, z, far_z, peer_z, at_z)
    gstat2[z] = sstat2[...]
    got2[z] = send2[z]
    arrived(sstat2, gstat2, t2, q2, far_z[::-1], peer_z, at_z)
    arrived(send2.at[0], got2, s2, r2, far_z[::-1], peer_z, at_z)
    top, total, value = merged(got2, gstat2, NZ)
    attn[z] = (value / total).astype(jnp.bfloat16)

    exchange(lambda p: attn.at[z], attn, s3, r3, z, far_z, peer_z, at_z)
    own_weight.wait()
    arrived(weight_ref.at[:, pl.ds(0, HD)], weights, sw, rw, far_j[::-1], peer_j, at_j)
    arrived(attn.at[0], attn, s3, r3, far_z[::-1], peer_z, at_z)

    whole = jnp.concatenate([attn[p] for p in range(NZ)], axis=0)
    for p in range(NJ):
        send4[p] = jnp.dot(weights[p], whole, preferred_element_type=jnp.float32).astype(jnp.bfloat16)
    exchange(lambda p: send4.at[p], got4, s4, r4, j, far_j, peer_j, at_j)
    got4[j] = send4[j]
    arrived(send4.at[0], got4, s4, r4, far_j[::-1], peer_j, at_j)
    part = functools.reduce(jnp.add, [got4[p].astype(jnp.float32) for p in range(NJ)])

    got5[x] = part.astype(jnp.bfloat16)
    exchange(lambda p: got5.at[x], got5, s5, r5, x, (2, 1, 3), peer_x, at_x)
    arrived(got5.at[0], got5, s5, r5, (1, 3, 2), peer_x, at_x)
    projected = functools.reduce(jnp.add, [got5[p].astype(jnp.float32) for p in range(NX)])

    got6[seq] = jnp.sum(projected * projected, axis=0, keepdims=True)
    exchange(lambda p: got6.at[seq], got6, s6, r6, seq, range(1, NS), peer_s, at_s)
    arrived(got6.at[0], got6, s6, r6, range(1, NS), peer_s, at_s)
    square = functools.reduce(jnp.add, [got6[p] for p in range(NS)])
    out_ref[...] = projected * lax.rsqrt(square * (1.0 / D) + 1e-06)

    for c in sends:
        c.wait_send()
    for k in range(1, NJ):
        p = peer_j(k)
        copy(stat_ref.at[p], gstat1.at[j], t1.at[p], q1.at[j], at_j(p)).wait_send()
        copy(acc_ref.at[p], got1.at[j], s1.at[p], r1.at[j], at_j(p)).wait_send()


def fused(length, query, key, value, weight):
    bf16, f32 = jnp.bfloat16, jnp.float32
    dma = pltpu.SemaphoreType.DMA
    j2, z2, x2, a2 = [dma((NJ,))] * 2, [dma((NZ,))] * 2, [dma((NX,))] * 2, [dma((NS,))] * 2
    vmem = pl.BlockSpec(memory_space=pltpu.VMEM)
    hbm = pl.BlockSpec(memory_space=pl.ANY)
    return pl.pallas_call(
        kernel,
        out_shape=jax.ShapeDtypeStruct((ROWS, TOK), f32),
        in_specs=[pl.BlockSpec(memory_space=pltpu.SMEM), vmem, hbm, hbm, hbm],
        out_specs=vmem,
        scratch_shapes=[
            pltpu.VMEM((KEYS * KV, HD), bf16),
            pltpu.VMEM((KEYS * KV, HD), bf16),
            pltpu.VMEM((KEYS * KV, HD), f32),
            pltpu.VMEM((KEYS * KV, HD), f32),
            pltpu.VMEM((TOK * NJ, HD), f32),
            pltpu.VMEM((NJ, HD, TOK), bf16),
            pltpu.VMEM((NJ, 2, TOK), f32),
            pltpu.VMEM((NJ, HD, TOK), bf16),
            pltpu.VMEM((NJ, 2, TOK), f32),
            pltpu.VMEM((NJ, ROWS, HD), bf16),
            pltpu.VMEM((NZ, DZ, TOK), bf16),
            pltpu.VMEM((2, TOK), f32),
            pltpu.VMEM((NZ, DZ, TOK), bf16),
            pltpu.VMEM((NZ, 2, TOK), f32),
            pltpu.VMEM((NZ, DZ, TOK), bf16),
            pltpu.VMEM((NJ, ROWS, TOK), bf16),
            pltpu.VMEM((NJ, ROWS, TOK), bf16),
            pltpu.VMEM((NX, ROWS, TOK), bf16),
            pltpu.VMEM((NS, 1, TOK), f32),
            dma((PARTS,)),
            dma((PARTS,)),
            dma(()),
            *j2, *j2, *j2, *z2, *z2, *z2, *j2, *x2, *a2,
        ],
        compiler_params=pltpu.CompilerParams(
            collective_id=0, has_side_effects=True, vmem_limit_bytes=60 * 2**20
        ),
    )(length, query, key, value, weight)


def body(query, key_cache, value_cache, lengths, out_weight, norm_gain):
    normed = fused(
        lengths,
        query.reshape(TOK * NJ, HD),
        key_cache.reshape(KEYS * KV, HD),
        value_cache.reshape(KEYS * KV, HD),
        out_weight,
    )
    return (normed * norm_gain[:, None]).astype(jnp.bfloat16).T


def solution(mesh):
    placed = (
        P(None, "head", None),
        P("seq", "head", None),
        P("seq", "head", None),
        P("seq"),
        P("seq", "head"),
        P("seq"),
    )
    return jax.shard_map(
        body, mesh=mesh, in_specs=placed, out_specs=P(None, "seq"), check_vma=False
    )
```

time: 56.8 us -> 48 us (0.85)
  matrix products: 7.28 us -> 0 us
  Pallas kernels: 42.1 us -> 45.7 us
  other arithmetic: 4.72 us -> 1.45 us
  local copies, waits for them, and re-layouts: 1.65 us -> 0.01 us
    dot_general x2 -> x0, matrix products: 7.28 us -> none  [the longest x1 3.84 us: body(): jnp.einsum('tkgd,ckd->kgtc', grouped, key_cache, preferred_element_type=j...]
    pallas_call x1, Pallas kernels: 42.1 us -> 45.7 us  [fused(): pl.pallas_call(kernel, out_shape=jax.ShapeDtypeStruct((ROWS, TOK), f32),...]
    reduce_sum x1 -> x0, other arithmetic: 2.65 us -> none  [body(): block_sum = jnp.sum(weights, axis=-1)]
    convert_element_type x1 -> x0, local copies, waits for them, and re-layouts: 0.84 us -> none  [body(): weighted.astype(jnp.bfloat16).reshape(heads_local, head_dim, tok_count)]
    unnamed x4 -> x2, local copies, waits for them, and re-layouts: 0.81 us -> 0.01 us
    another operation x1 -> x0, other arithmetic: 0.61 us -> none  [body(): jnp.stack([block_max, block_sum], axis=2).reshape(heads_local, 2, tok_count)]
where the time goes in v2:
time: 48 us; the launch traced here: 47.9 us
  Pallas kernels  45.7 us (95%)
  other arithmetic  1.45 us (3%)
  between operations  0.68 us (1%)
    pallas_call x1, Pallas kernels, fused(): pl.pallas_call(kernel, out_shape=jax.ShapeDtypeStruct((ROWS, TOK), f32),...  45.7 us
    transpose x1, other arithmetic, body(): return (normed * norm_gain[:, None]).astype(jnp.bfloat16).T  1.45 us

profile of v2, /device:TPU:1, one launch (start us, length us, event | category | flops | bytes accessed | tf_op | source)
XLA Modules:
  0.0 47.9 jit_solution(11465964019807709683)
XLA Ops:
  0.7 0.0 copy-start
  0.7 45.7 %shard_map.64 = f32[72,128]{1,0:T(8,128)} custom-call(s32[1]{0:T(128)S(6)} %copy.7.length_ref, bf16[1024,128]{1,0:T(8,128)(2,1)} %bitcast.7, bf16[8192,128]{1,0:T(8,128)(2,1)} %bitcast.5, bf16[8192,128]{1,0:T(8,128)(2,1)} %bitcast.6, bf16[72,1024]{1,0:T(8,128)(2,1)} %weight_ref.1), custom_call_target="tpu_custom_call" | custom-call | tf_op jit(solution)/shard_map/pallas_call | solution.py:267
  46.4 0.0 copy-done
  46.4 1.5 %fusion = bf16[128,72]{0,1:T(8,128)(2,1)} fusion(f32[72,128]{1,0:T(8,128)} %shard_map.64, f32[72]{0:T(128)S(1)} %copy-done), kind=kLoop, calls=%fused_computation.1 | loop fusion | flops 18432 | bytes 55584 | tf_op jit(solution)/shard_map/transpose | solution.py:311
Async XLA Ops:
  0.7 45.8 %copy-start = (f32[72]{0:T(128)S(1)}, f32[72]{0:T(128)}, u32[]{:S(2)}) copy-start(f32[72]{0:T(128)} %param.11) | copy-start | bytes 868
